TPU v7x, 256 devices: a whole 4x4x8 slice. The times are simulated.
256 devices in a mesh: outer: 8 (over x, y_hi), dp: 32 (over y_lo, z, core).
Axes of the slice: x: 4, y: 4 (y_hi: 2, y_lo: 2; y = y_hi * 2 + y_lo), z: 8, core: 2. Of those that a mesh axis runs over, the one named last changes fastest.
Arguments:
- fast_weights: float32 [8, 4096, 2048], P('outer', 'dp'), may hold values from -6 to 6
- slow_weights: float32 [4096, 2048], P('dp', 'outer'), may hold values from -6 to 6
- momentum: float32 [4096, 2048], P('dp', 'outer'), may hold values from -3 to 3
- tokens: bfloat16 [196608, 4096], P(('outer', 'dp')), may hold values from -6 to 6
- norm_gain: float32 [4096], replicated, may hold values from 0.1 to 1.9
Outputs:
- slow_next: float32 [4096, 2048], P('dp', 'outer')
- momentum_next: float32 [4096, 2048], P('dp', 'outer')
- fast_next: float32 [4096, 2048], P('dp')
- key_values: bfloat16 [196608, 2048], P(('outer', 'dp'))
All inputs are finite; a program needn't handle non-finite values.
Results may differ from a plain program's by a relative error of at most 0.0057.
Values may be sent and summed in bfloat16 or wider, within the bound.
A program may use at most 128 MiB of HBM per device.

v0:
```python
import jax
import jax.numpy as jnp
from jax import lax
from jax.sharding import PartitionSpec as P

OUTER_LR = 0.7
MOMENTUM_COEF = 0.9
EPSILON = 1e-05


def cut_along(shard, dim, size):
    before, after = (shard.shape[:dim], shard.shape[dim + 1 :])
    return jnp.moveaxis(shard.reshape(*before, size, -1, *after), dim, 0)


def summed_on_arrival(shard, axis, dim):
    parts = cut_along(shard, dim, lax.axis_size(axis))
    arrived = lax.all_to_all(parts, axis, split_axis=0, concat_axis=0, tiled=True)
    return arrived.sum(axis=0)


def in_order(parts, dim):
    lengths = list(parts.shape[1:])
    lengths[dim] *= parts.shape[0]
    return jnp.moveaxis(parts, 0, dim).reshape(lengths)


def sent_to_all(shard, axis):
    copies = jnp.broadcast_to(shard, (lax.axis_size(axis), *shard.shape))
    return lax.all_to_all(copies, axis, split_axis=0, concat_axis=0, tiled=True)


def collect(shard, axis, dim):
    return in_order(sent_to_all(shard, axis), dim)


def outer_update(slow_part, moment_part, fast_total, pod_count):
    outer_grad = slow_part - fast_total / pod_count
    moment_next = MOMENTUM_COEF * moment_part + outer_grad
    slow_next = slow_part - OUTER_LR * (outer_grad + MOMENTUM_COEF * moment_next)
    return (slow_next, moment_next)


def body(fast_weights, slow_weights, momentum, tokens, norm_gain):
    pod_count = lax.axis_size("outer")
    width = tokens.shape[1]
    fast_total = summed_on_arrival(fast_weights[0], "outer", 1)
    slow_next, momentum_next = outer_update(slow_weights, momentum, fast_total, pod_count)
    fast_next = collect(slow_next, "outer", 1)
    values = tokens.astype(jnp.float32)
    meansq = jnp.mean(values * values, axis=-1, keepdims=True)
    normed = (values * lax.rsqrt(meansq + EPSILON) * norm_gain).astype(jnp.bfloat16)
    whole_weights = lax.all_gather(fast_next.astype(jnp.bfloat16), "dp", axis=0, tiled=True)
    product = jnp.dot(normed, whole_weights, preferred_element_type=jnp.float32)
    key_values = (product * width ** (-0.5)).astype(jnp.bfloat16)
    return (slow_next, momentum_next, fast_next, key_values)


def solution(mesh):
    in_specs = (
        P("outer", "dp", None),
        P("dp", "outer"),
        P("dp", "outer"),
        P(("outer", "dp"), None),
        P(),
    )
    out_specs = (P("dp", "outer"), P("dp", "outer"), P("dp", None), P(("outer", "dp"), None))
    return jax.shard_map(body, mesh=mesh, in_specs=in_specs, out_specs=out_specs, check_vma=False)
```

profile of v0, /device:TPU:1, one launch (start us, length us, event | category | flops | bytes accessed | tf_op | source)
XLA Modules:
  0.0 205.2 jit_solution(3373704709159486115)
XLA Ops:
  7.2 0.0 copy-start.1
  7.2 0.0 all-gather.2.cloned.1.call-start
  7.2 1.5 copy.9
  8.8 0.3 copy.10
  9.1 22.6 %all_to_all.10 = f32[8,128,256]{2,1,0:T(8,128)S(1)} all-to-all(f32[8,128,256]{2,1,0:T(8,128)S(1)} %copy.10), channel_id=1, replica_groups=mesh['outer'=8,'dp'=32] {'outer'}, dimensions={0} | all-to-all | bytes 2097152 | tf_op jit(solution)/shard_map/all_to_all | solution.py:18
  31.7 0.1 reduce_sum.18
  31.8 1.7 multiply_subtract_fusion
  33.5 0.0 copy-start
  33.5 0.1 broadcast_in_dim.2
  33.6 17.5 %all_to_all.11 = f32[8,128,256]{2,1,0:T(8,128)S(1)} all-to-all(f32[8,128,256]{2,1,0:T(8,128)S(1)} %broadcast_in_dim.2), channel_id=1, replica_groups=mesh['outer'=8,'dp'=32] {'outer'}, dimensions={0} | all-to-all | bytes 2097152 | tf_op jit(solution)/shard_map/all_to_all | solution.py:30
  51.1 0.3 copy.11
  51.4 0.9 bitcast_convert_fusion
  52.2 0.0 all-gather.2.cloned.1.call-update
  52.3 4.1 %fusion = f32[768]{0:T(1024)S(1)} fusion(bf16[768,4096]{1,0:T(8,128)(2,1)} %param.8), kind=kLoop, calls=%fused_computation.2 | loop fusion | flops 9436416 | bytes 6294528 | tf_op jit(solution)/shard_map/reduce_sum | solution.py:51
  56.4 1.3 copy.12
  57.7 120.9 %all-gather.2.cloned.1.call-done = bf16[4096,2048]{0,1:T(8,128)(2,1)} async-done(((bf16[128,2048]{0,1:T(8,128)(2,1)}), bf16[4096,2048]{0,1:T(8,128)(2,1)}) %all-gather.2.cloned.1.call-update) | async-done | bytes 16777232 | tf_op jit(solution)/shard_map/all_gather | solution.py:53
  178.6 0.0 copy-done.1
  178.6 19.7 %multiply_convert_fusion = bf16[768,2048]{1,0:T(8,128)(2,1)} fusion(bf16[4096,2048]{0,1:T(8,128)(2,1)} %all-gather.2.cloned.1.call-done, bf16[768,4096]{1,0:T(8,128)(2,1)} %param.8, f32[4096]{0:T(1024)S(1)} %copy-done.1, f32[768]{0:T(1024)S(1)} %add_rsqrt_fusion), kind=kOutput, calls=%fused_computation.6 | convolution fusion | flops 12900630528 | bytes 26233856 | tf_op jit(solution)/shard_map/dot_general | solution.py:54
  198.3 0.0 copy-done
  (1 shorter events, 0.0 us)
Async XLA Ops:
  7.2 171.4 %copy-start.1 = (f32[4096]{0:T(1024)S(1)}, f32[4096]{0:T(1024)}, u32[]{:S(2)}) copy-start(f32[4096]{0:T(1024)} %param.9) | copy-start | bytes 49156
  7.2 171.4 %all-gather.2.cloned.1.call-start = ((), (), s32[]{:S(2)}) async-start(), calls=%async_computation.2 | async-start | bytes 17301504 | tf_op jit(solution)/shard_map/all_gather | solution.py:53
  33.5 164.8 %copy-start = (f32[128,256]{1,0:T(8,128)}, f32[128,256]{1,0:T(8,128)S(1)}, u32[]{:S(2)}) copy-start(f32[128,256]{1,0:T(8,128)S(1)} %get-tuple-element.8) | copy-start | bytes 393220
Sparse Core Ops, SparseCore 0:
  52.4 126.1 all-gather.1
where the time goes:
time: 207 us; the launch traced here: 205 us
  waiting for transfers between devices  121 us (58%)
  blocking collectives  40.1 us (19%)
  matrix products  19.7 us (10%)
  between operations  14.1 us (7%)
  other arithmetic  6.66 us (3%)
  local copies, waits for them, and re-layouts  3.61 us (2%)
    all_gather x1, waiting for transfers between devices, body(): lax.all_gather(fast_next.astype(jnp.bfloat16), 'dp', axis=0, tiled=True)  121 us
    all_to_all x1, blocking collectives, summed_on_arrival(): lax.all_to_all(parts, axis, split_axis=0, concat_axis=0, tiled=True)  22.6 us
    dot_general x1, matrix products, body(): product = jnp.dot(normed, whole_weights, preferred_element_type=jnp.float32)  19.7 us
    all_to_all x1, blocking collectives, sent_to_all(): return lax.all_to_all(copies, axis, split_axis=0, concat_axis=0, tiled=True)  17.5 us
  transfers between devices with their start and end apart: 1, of which 1 were waited for; matrix products, arithmetic and copies ran while one was open for 3% of the time, Pallas kernels for 0%

commit v1 on v0

v1 whole, which is shorter than its diff:
```python
import heapq

import jax
import jax.numpy as jnp
from jax import lax
from jax.experimental import pallas as pl
from jax.experimental.pallas import tpu as pltpu
from jax.sharding import PartitionSpec as P

OUTER_LR = 0.7
MOMENTUM_COEF = 0.9
EPSILON = 1e-05
MESH = pl.DeviceIdType.MESH

NX, NY, NZ = 4, 4, 8
SIZES = dict(x=NX, y=NY, z=NZ)
WAVES = 2
LANES = 128
COLOURS = (
    (("x", "y", "z"), (0, 48), (0, 48)),
    (("z", "y", "x"), (48, 96), (48, 80)),
    (("z", "x", "y"), (96, 128), (80, 128)),
)
LINK = 45.5
HOP, FURTHER = 1.9, 0.75
READY = (0.0, 3.5)


def spans(order, wave, colour):
    lo, hi = COLOURS[colour][1 + wave]
    return hi - lo


class Piece:
    def __init__(self, wave, colour, where):
        self.wave, self.colour, self.where = wave, colour, dict(where)

    def moved(self, axis, step):
        where = dict(self.where)
        where[axis] = (where[axis] - step) % SIZES[axis]
        return Piece(self.wave, self.colour, where)

    def cut(self, axis, half):
        where = dict(self.where)
        lo, hi = where[axis]
        mid = (lo + hi) // 2
        where[axis] = (lo, mid) if half == 0 else (mid, hi)
        return Piece(self.wave, self.colour, where)

    def key(self):
        return (self.wave, self.colour, tuple(sorted(self.where.items())))

    def kib(self):
        tiles = 1
        for span in self.where.values():
            if isinstance(span, tuple):
                tiles *= span[1] - span[0]
        return tiles * spans(None, self.wave, self.colour) * LANES * 2 / 1024


def ring_steps(size):
    far = size // 2
    steps = []
    for k in range(far):
        half = (0, 1) if k == far - 1 else (None, None)
        steps.append(((1, (-k) % size, half[0]), (-1, k % size, half[1])))
    return steps


def make_plan():
    free, heap, order, serial = {}, [], [], [0]
    have, followers = {}, {}

    def send(now, actions, piece, axis, step, phase):
        kib = piece.kib()
        hops = abs(step)
        link = (axis, step > 0)
        begin = max(now, free.get(link, 0.0))
        free[link] = begin + kib * hops / LINK
        arrive = begin + kib / LINK + HOP + FURTHER * (hops - 1)
        got = piece.moved(axis, step)
        index = serial[0]
        serial[0] += 1
        actions.append((piece, axis, step, phase, index))
        heapq.heappush(heap, (arrive, index, got, axis, phase, step))

    def spread(now, actions, base, axis, phase, offset, halves_axis, done_from):
        for pair in ring_steps(SIZES[axis]):
            for direction, held, half in pair:
                if held != offset:
                    continue
                if offset != 0 and done_from != direction:
                    continue
                piece = base if half is None else base.cut(halves_axis, half)
                send(now, actions, piece, axis, direction, phase)

    starts = []
    for wave in range(WAVES):
        heapq.heappush(heap, (READY[wave], -1 - wave, None, None, 0, wave))
    arrived = {}
    while heap:
        now, index, got, axis, phase, step = heapq.heappop(heap)
        actions, local = [], []
        if phase == 0:
            wave = step
            for colour, (axes, *_r) in enumerate(COLOURS):
                own = Piece(wave, colour, dict(x=0, y=0, z=0))
                a = axes[0]
                size = SIZES[a]
                for distance in range(1, size // 2 + 1):
                    for sign in (1, -1):
                        if distance == size // 2 and sign == -1:
                            continue
                        send(now, actions, own, a, sign * distance, 1)
            order.append((now, "ready", wave, None, actions, local, None))
            continue
        wave, colour = got.wave, got.colour
        a, b, c = COLOURS[colour][0]
        if phase == 1:
            tag = (wave, colour, 1)
            arrived[tag] = arrived.get(tag, 0) + 1
            if arrived[tag] == SIZES[a] - 1:
                where = {a: (0, SIZES[a]), b: 0, c: 0}
                line = Piece(wave, colour, where)
                spread(now, actions, line, b, 2, 0, a, None)
                spread(now, actions, line, c, 3, 0, a, None)
                local.append(line)
        elif phase == 2:
            offset = got.where[b]
            span = got.where[a]
            whole = span == (0, SIZES[a])
            if whole:
                spread(now, actions, got, b, 2, offset, a, step)
            full = Piece(wave, colour, {**got.where, a: (0, SIZES[a])})
            tag = full.key()
            arrived[tag] = arrived.get(tag, 0) + (2 if whole else 1)
            if arrived[tag] == 2:
                spread(now, actions, full, c, 3, 0, a, None)
                local.append(full)
        else:
            if got.where[a] == (0, SIZES[a]):
                spread(now, actions, got, c, 3, got.where[c], a, step)
            local.append(got)
        order.append((now, "recv", wave, got, actions, local, index))
    return order, serial[0]


PLAN, COPIES = make_plan()


def kernel(fast_in, slow_in, moment_in, tokens_in, gain_in,
           slow_out, moment_out, fast_out, kv_out,
           tiles, fast, outgoing, incoming, slow, moment, tokens, gain, slow_new, moment_new, fast_new, total, product,
           load_sem, store_sem, rs_send, rs_recv, ag_send, ag_recv, pair_send, pair_recv):
    outer, dp = lax.axis_index("outer"), lax.axis_index("dp")
    x, yh = outer // 2, outer % 2
    yl, z, core = dp // 16, (dp // 2) % NZ, dp % 2
    y = yh * 2 + yl
    here = dict(x=x, y=y, z=z)
    other = 1 - core

    def device(px, py, pz, pc):
        return (px * 2 + py // 2, (py % 2) * 16 + pz * 2 + pc)

    def beside(axis, step):
        at = dict(here)
        at[axis] = lax.rem(at[axis] + (step % SIZES[axis]), SIZES[axis])
        return device(at["x"], at["y"], at["z"], core)

    partner = device(x, y, z, other)

    loads = [
        pltpu.make_async_copy(fast_in.at[0], fast, load_sem.at[0]),
        pltpu.make_async_copy(slow_in, slow, load_sem.at[1]),
        pltpu.make_async_copy(moment_in, moment, load_sem.at[2]),
        pltpu.make_async_copy(gain_in, gain, load_sem.at[3]),
        pltpu.make_async_copy(tokens_in, tokens, load_sem.at[4]),
    ]
    for load in loads:
        load.start()

    peers = []
    for dx in range(NX):
        for dy in (0, 2):
            if dx or dy:
                peers.append(device(lax.rem(x + dx, NX), lax.rem(y + dy, NY), z, core))
    greet = list(peers) + [partner, beside("y", 1), beside("y", -1)] + [beside("z", s) for s in range(1, NZ)]
    barrier = pltpu.get_barrier_semaphore()
    for peer in greet:
        pl.semaphore_signal(barrier, inc=1, device_id=peer, device_id_type=MESH)

    loads[0].wait()
    for wave in range(WAVES):
        for o in range(NX * 2):
            outgoing[wave, o] = fast[:, o * 256 + wave * LANES:o * 256 + (wave + 1) * LANES].astype(jnp.bfloat16)
    loads[1].wait()
    loads[2].wait()
    loads[3].wait()
    pl.semaphore_wait(barrier, len(greet))

    for wave in range(WAVES):
        for index, peer in enumerate(peers):
            pltpu.make_async_remote_copy(
                src_ref=outgoing.at[wave, peer[0]], dst_ref=incoming.at[wave, outer],
                send_sem=rs_send.at[wave], recv_sem=rs_recv.at[wave], device_id=peer, device_id_type=MESH).start()

    def norm_rows(first, count):
        @pl.loop(first, first + count)
        def _(i):
            rows = pl.ds(i * 16, 16)
            values = tokens[rows, :].astype(jnp.float32)
            meansq = jnp.mean(values * values, axis=-1, keepdims=True)
            tokens[rows, :] = (values * lax.rsqrt(meansq + EPSILON) * gain[...]).astype(jnp.bfloat16)

    def rs_wait(wave):
        landed = incoming.at[wave, 0:7]
        pltpu.make_async_remote_copy(
            src_ref=landed, dst_ref=landed, send_sem=rs_send.at[wave], recv_sem=rs_recv.at[wave],
            device_id=partner, device_id_type=MESH).wait_recv()

    def update(wave):
        cols = slice(wave * LANES, (wave + 1) * LANES)
        summed = fast[:, pl.ds(pl.multiple_of(outer * 256 + wave * LANES, LANES), LANES)]
        for k in range(1, NX * 2):
            summed = summed + incoming[wave, lax.rem(outer + k, NX * 2)].astype(jnp.float32)
        part = slow[:, cols]
        outer_grad = part - summed / (NX * 2)
        moment_next = MOMENTUM_COEF * moment[:, cols] + outer_grad
        slow_next = part - OUTER_LR * (outer_grad + MOMENTUM_COEF * moment_next)
        tiles[wave, x, y, z, core] = slow_next.astype(jnp.bfloat16)
        slow_new[:, cols] = slow_next
        moment_new[:, cols] = moment_next

    def slice_of(piece):
        lo, hi = COLOURS[piece.colour][1 + piece.wave]
        index = [piece.wave]
        for axis in ("x", "y", "z"):
            span = piece.where[axis]
            if isinstance(span, tuple):
                index.append(slice(span[0], span[1]))
            else:
                index.append(lax.rem(here[axis] + span, SIZES[axis]) if span else here[axis])
        return tiles.at[(*index, core, slice(lo, hi), slice(None))]

    def ag_copy(piece, axis, step, phase, index):
        ref = slice_of(piece)
        return pltpu.make_async_remote_copy(
            src_ref=ref, dst_ref=ref, send_sem=ag_send.at[piece.wave, piece.colour, phase - 1], recv_sem=ag_recv.at[index],
            device_id=beside(axis, step), device_id_type=MESH)

    def pair_copy(ref, wave):
        return pltpu.make_async_remote_copy(
            src_ref=ref, dst_ref=ref, send_sem=pair_send.at[wave], recv_sem=pair_recv.at[wave],
            device_id=partner, device_id_type=MESH)

    def matmul(wave, px, part):
        yl_part, zs = part // 2, slice((part % 2) * 4, (part % 2) * 4 + 4)
        left = tiles[wave, px, yl_part, zs].reshape(1024, LANES)
        right = tiles[wave, px, 2 + yl_part, zs].reshape(1024, LANES)
        weights = jnp.concatenate([left, right], axis=1)

        @pl.loop(0, 3)
        def _(m):
            rows = pl.ds(m * 256, 256)
            value = jnp.dot(tokens[rows, part * 1024:(part + 1) * 1024], weights, preferred_element_type=jnp.float32)
            if part == 0:
                total[rows, :] = value
            elif part < 3:
                total[rows, :] += value
            else:
                value = ((total[rows, :] + value) * (4096 ** -0.5)).astype(jnp.bfloat16)
                product[wave, px, 0, rows, :] = value[:, :LANES]
                product[wave, px, 1, rows, :] = value[:, LANES:]

    stores = []

    def store(src, dst, index):
        copy = pltpu.make_async_copy(src, dst, store_sem.at[index])
        copy.start()
        stores.append(copy)

    def finish_columns(wave, px):
        for h in range(2):
            o = px * 2 + h
            cols = slice(o * 256 + wave * LANES, o * 256 + (wave + 1) * LANES)
            store(product.at[wave, px, h], kv_out.at[:, cols], 3 + (wave * 4 + px) * 2 + h)

    def own_rows(wave):
        for o in range(NX * 2):
            cols = slice(o * 256 + wave * LANES, o * 256 + (wave + 1) * LANES)
            rounded = tiles[wave, o // 2, (o % 2) * 2 + yl, z, core].astype(jnp.float32)
            exact = slow_new[:, wave * LANES:(wave + 1) * LANES]
            fast_new[:, cols] = jnp.where(jnp.full((128, LANES), o, jnp.int32) == outer, exact, rounded)

    def wave_done(wave):
        ref = tiles.at[wave, :, :, :, other]
        pltpu.make_async_remote_copy(
            src_ref=ref, dst_ref=ref, send_sem=pair_send.at[wave], recv_sem=pair_recv.at[wave],
            device_id=partner, device_id_type=MESH).wait_recv()

    loads[4].wait()
    norm_rows(0, 16)
    remaining = {0: 0, 1: 0}
    for event in PLAN:
        if event[1] == "recv":
            remaining[event[2]] += 1
    work = []
    for number, (now, kind, wave, got, actions, local, index) in enumerate(PLAN):
        if kind == "ready":
            rs_wait(wave)
            update(wave)
        else:
            ref = slice_of(got)
            pltpu.make_async_remote_copy(
                src_ref=ref, dst_ref=ref, send_sem=ag_send.at[0, 0, 0], recv_sem=ag_recv.at[index],
                device_id=partner, device_id_type=MESH).wait_recv()
        for action in actions:
            ag_copy(*action).start()
        for piece in local:
            pair_copy(slice_of(piece), wave).start()
        if kind == "ready":
            norm_rows(16 + 16 * wave, 16)
            if wave == 1:
                store(slow_new, slow_out, 0)
                store(moment_new, moment_out, 1)
            continue
        remaining[wave] -= 1
        if remaining[wave] == 0:
            if wave == 0:
                wave_done(0)
                for px in range(NX):
                    for part in range(4):
                        work.append((px, part))
            else:
                while work:
                    px, part = work.pop(0)
                    matmul(0, px, part)
                    if part == 3:
                        finish_columns(0, px)
                own_rows(0)
                own_rows(1)
                store(fast_new, fast_out, 2)
                wave_done(1)
                for px in range(NX):
                    for part in range(4):
                        matmul(1, px, part)
                    finish_columns(1, px)
        elif work:
            px, part = work.pop(0)
            matmul(0, px, part)
            if part == 3:
                finish_columns(0, px)

    for copy in stores:
        copy.wait()
    for wave in range(WAVES):
        sent = incoming.at[wave, 0:7]
        pltpu.make_async_remote_copy(
            src_ref=sent, dst_ref=sent, send_sem=rs_send.at[wave], recv_sem=rs_recv.at[wave],
            device_id=partner, device_id_type=MESH).wait_send()
        sent = tiles.at[wave, :, :, :, core]
        pltpu.make_async_remote_copy(
            src_ref=sent, dst_ref=sent, send_sem=pair_send.at[wave], recv_sem=pair_recv.at[wave],
            device_id=partner, device_id_type=MESH).wait_send()
        for colour, (axes, *_r) in enumerate(COLOURS):
            lo, hi = COLOURS[colour][1 + wave]
            a, b, c = axes
            ranges = (
                {a: slice(0, SIZES[a] - 1), b: 0, c: 0},
                {a: slice(0, SIZES[a]), b: slice(0, SIZES[b] - 1), c: 0},
                {a: slice(0, SIZES[a]), b: slice(0, SIZES[b]), c: slice(0, SIZES[c] - 1)},
            )
            for phase, span in enumerate(ranges):
                sent = tiles.at[wave, span["x"], span["y"], span["z"], core, lo:hi, :]
                pltpu.make_async_remote_copy(
                    src_ref=sent, dst_ref=sent, send_sem=ag_send.at[wave, colour, phase], recv_sem=ag_recv.at[0],
                    device_id=partner, device_id_type=MESH).wait_send()


def body(fast_weights, slow_weights, momentum, tokens, norm_gain):
    rows, cols = slow_weights.shape
    count, width = tokens.shape
    whole = fast_weights.shape[2]
    hbm = pl.BlockSpec(memory_space=pl.ANY)
    dma = pltpu.SemaphoreType.DMA
    return pl.pallas_call(
        kernel,
        out_shape=(
            jax.ShapeDtypeStruct((rows, cols), jnp.float32),
            jax.ShapeDtypeStruct((rows, cols), jnp.float32),
            jax.ShapeDtypeStruct((rows, whole), jnp.float32),
            jax.ShapeDtypeStruct((count, whole), jnp.bfloat16),
        ),
        in_specs=[hbm] * 5,
        out_specs=(hbm,) * 4,
        scratch_shapes=[
            pltpu.VMEM((WAVES, NX, NY, NZ, 2, 128, LANES), jnp.bfloat16),
            pltpu.VMEM((rows, whole), jnp.float32),
            pltpu.VMEM((WAVES, 8, rows, LANES), jnp.bfloat16),
            pltpu.VMEM((WAVES, 8, rows, LANES), jnp.bfloat16),
            pltpu.VMEM((rows, cols), jnp.float32),
            pltpu.VMEM((rows, cols), jnp.float32),
            pltpu.VMEM((count, width), jnp.bfloat16),
            pltpu.VMEM((1, width), jnp.float32),
            pltpu.VMEM((rows, cols), jnp.float32),
            pltpu.VMEM((rows, cols), jnp.float32),
            pltpu.VMEM((rows, whole), jnp.float32),
            pltpu.VMEM((count, 256), jnp.float32),
            pltpu.VMEM((WAVES, NX, 2, count, LANES), jnp.bfloat16),
            dma((5,)),
            dma((19,)),
            dma((WAVES,)),
            dma((WAVES,)),
            dma((WAVES, 3, 3)),
            dma((COPIES,)),
            dma((WAVES,)),
            dma((WAVES,)),
        ],
        compiler_params=pltpu.CompilerParams(collective_id=0, has_side_effects=True, vmem_limit_bytes=60 * 1024 * 1024),
    )(fast_weights, slow_weights, momentum, tokens, norm_gain.reshape(1, width))


def solution(mesh):
    in_specs = (
        P("outer", "dp", None),
        P("dp", "outer"),
        P("dp", "outer"),
        P(("outer", "dp"), None),
        P(),
    )
    out_specs = (P("dp", "outer"), P("dp", "outer"), P("dp", None), P(("outer", "dp"), None))
    return jax.shard_map(body, mesh=mesh, in_specs=in_specs, out_specs=out_specs, check_vma=False)
```

time: 207 us -> 102 us (0.49)
  waiting for transfers between devices: 121 us -> 0 us
  Pallas kernels: 0 us -> 91.5 us
  blocking collectives: 40.1 us -> 0 us
  matrix products: 19.7 us -> 0 us
  between operations: 14.1 us -> 0.64 us
  other arithmetic: 6.66 us -> 0 us
  local copies, waits for them, and re-layouts: 3.61 us -> 9.4 us
    all_gather x1 -> x0, waiting for transfers between devices: 121 us -> none  [body(): lax.all_gather(fast_next.astype(jnp.bfloat16), 'dp', axis=0, tiled=True)]
    pallas_call x0 -> x1, Pallas kernels: none -> 91.5 us  [body(): pl.pallas_call(kernel, out_shape=(jax.ShapeDtypeStruct((rows, cols), jnp....]
    all_to_all x2 -> x0, blocking collectives: 40.1 us -> none  [the longest x1 22.6 us: summed_on_arrival(): lax.all_to_all(parts, axis, split_axis=0, concat_axis=0, tiled=True)]
    dot_general x1 -> x0, matrix products: 19.7 us -> none  [body(): product = jnp.dot(normed, whole_weights, preferred_element_type=jnp.float32)]
    unnamed x6 -> x4, local copies, waits for them, and re-layouts: 2.87 us -> 9.4 us
    reduce_sum x2 -> x0, other arithmetic: 4.14 us -> none  [the longest x1 4.08 us: body(): meansq = jnp.mean(values * values, axis=-1, keepdims=True)]
  transfers between devices with their start and end apart: 1 -> 0, of which waited for: 1 -> 0; matrix products, arithmetic and copies ran while one was open for 3% -> 0% of each run, Pallas kernels for 0% -> 0%
where the time goes in v1:
time: 102 us
  Pallas kernels  91.5 us (90%)
  local copies, waits for them, and re-layouts  9.4 us (9%)
    pallas_call x1, Pallas kernels, body(): pl.pallas_call(kernel, out_shape=(jax.ShapeDtypeStruct((rows, cols), jnp....  91.5 us
    unnamed x4, local copies, waits for them, and re-layouts  9.4 us

profile of v1, /device:TPU:1, one launch (start us, length us, event | category | flops | bytes accessed | tf_op | source)
XLA Modules:
  0.0 101.5 jit_solution(14327381907486382372)
XLA Ops:
  0.6 91.5 %shard_map.84 = (f32[128,256]{1,0:T(8,128)}, f32[128,256]{1,0:T(8,128)}, f32[128,2048]{1,0:T(8,128)}, bf16[768,2048]{1,0:T(8,128)(2,1)}) custom-call(f32[1,128,2048]{2,1,0:T(8,128)} %fast_in.1, f32[128,256]{1,0:T(8,128)} %slow_in.1, f32[128,256]{1,0:T(8,128)} %moment_in.1, bf16[768,4096]{1,0:T(8,128)(2,1)} %tokens_in.1, f32[1,4096]{1,0:T(1,128)} %bitcast.1), custom_call_target="tpu_custom_call" | custom-call | tf_op jit(solution)/shard_map/pallas_call | solution.py:386
  92.1 1.6 %copy.13 = f32[128,256]{1,0:T(8,128)} copy(f32[128,256]{1,0:T(8,128)} %get-tuple-element.8) | data formatting | bytes 262144
  93.7 1.6 %copy.14 = f32[128,256]{1,0:T(8,128)} copy(f32[128,256]{1,0:T(8,128)} %get-tuple-element.9) | data formatting | bytes 262144
  95.3 2.3 %copy.15 = f32[128,2048]{1,0:T(8,128)} copy(f32[128,2048]{1,0:T(8,128)} %get-tuple-element.10) | data formatting | bytes 2097152
  97.6 4.0 %copy.16 = bf16[768,2048]{1,0:T(8,128)(2,1)} copy(bf16[768,2048]{1,0:T(8,128)(2,1)} %get-tuple-element.11) | data formatting | bytes 6291456

commit v2 on v1

v2 whole, which is shorter than its diff:
```python
import heapq

import jax
import jax.numpy as jnp
from jax import lax
from jax.experimental import pallas as pl
from jax.experimental.pallas import tpu as pltpu
from jax.sharding import PartitionSpec as P

OUTER_LR = 0.7
MOMENTUM_COEF = 0.9
EPSILON = 1e-05
MESH = pl.DeviceIdType.MESH

NX, NY, NZ = 4, 4, 8
SIZES = dict(x=NX, y=NY, z=NZ)
WAVES = 2
STEPS = 1
LANES = 128
COLOURS = (
    (("x", "y", "z"), (0, 48), (0, 32)),
    (("z", "y", "x"), (48, 80), (32, 80)),
    (("z", "x", "y"), (80, 128), (80, 128)),
)
MODES = (("dr", "dr", "dr"), ("dr", "dr", "dr"))
LINK = 45.5
HOP, FURTHER = 2.7, 0.75
READY = (0.0, 4.5)
BUSY = 0.0
CHUNK, PAIR = 1.05, 3.0
CHUNKS = [(pair, dy) for dy in (0, 3, 1, 2) for pair in ((0, 1), (3, 2))]


def spans(order, wave, colour):
    lo, hi = COLOURS[colour][1 + wave]
    return hi - lo


class Piece:
    def __init__(self, wave, colour, where):
        self.wave, self.colour, self.where = wave, colour, dict(where)

    def moved(self, axis, step):
        where = dict(self.where)
        where[axis] = (where[axis] - step) % SIZES[axis]
        return Piece(self.wave, self.colour, where)

    def cut(self, axis, half):
        where = dict(self.where)
        lo, hi = where[axis]
        mid = (lo + hi) // 2
        where[axis] = (lo, mid) if half == 0 else (mid, hi)
        return Piece(self.wave, self.colour, where)

    def key(self):
        return (self.wave, self.colour, tuple(sorted(self.where.items())))

    def tiles(self):
        spans = [range(*v) if isinstance(v, tuple) else [v] for v in (self.where[a] for a in "xyz")]
        return [(x, y, z) for x in spans[0] for y in spans[1] for z in spans[2]]

    def kib(self):
        tiles = 1
        for span in self.where.values():
            if isinstance(span, tuple):
                tiles *= span[1] - span[0]
        return tiles * spans(None, self.wave, self.colour) * LANES * 2 / 1024


def make_plan():
    free, heap, order, serial = {(a, s): BUSY for a in "xy" for s in (True, False)}, [], [], [0]
    arrived, missing, core = {}, {}, 0.0
    for wave in range(WAVES):
        for chunk in CHUNKS:
            missing[wave, chunk] = {(c, x, chunk[1], z) for c in range(3) for x in chunk[0] for z in range(NZ)}
    waiting = []
    turn = [(w, c) for w in range(WAVES) for c in CHUNKS]

    def landed(now, wave, piece):
        covered = {(piece.colour, *tile) for tile in piece.tiles()}
        for chunk in CHUNKS:
            left = missing[wave, chunk]
            if left:
                left -= covered
                if not left:
                    waiting.append((now + PAIR, wave, chunk))

    def send(now, actions, piece, axis, step, phase, offset, weight):
        kib, hops, link = piece.kib(), abs(step), (axis, step > 0)
        begin = max(now, free.get(link, 0.0))
        free[link] = begin + kib * hops / LINK
        index = serial[0]
        serial[0] += 1
        actions.append((piece, axis, step, phase, index))
        arrive = begin + kib / LINK + HOP + FURTHER * (hops - 1)
        heapq.heappush(heap, (arrive, index, piece.moved(axis, step), axis, phase, step, offset, weight))

    def start(now, actions, piece, axis, phase):
        far = SIZES[axis] // 2
        direct = phase < 3 and MODES[piece.wave][piece.colour][phase - 1] == "d"
        if not direct:
            for sign in (1, -1):
                send(now, actions, piece, axis, sign, phase, sign, 2)
            return
        for distance in range(1, far):
            for sign in (1, -1):
                send(now, actions, piece, axis, sign * distance, phase, sign * distance, 2)
        if phase == 1:
            sign = 1 if (piece.wave + piece.colour) % 2 else -1
            send(now, actions, piece, axis, sign * far, phase, far, 2)
        else:
            for half, sign in enumerate((1, -1)):
                send(now, actions, piece.cut(COLOURS[piece.colour][0][0], half), axis, sign * far, phase, far, 1)

    def forward(now, actions, got, axis, phase, offset, weight):
        if weight == 1 or (phase < 3 and MODES[got.wave][got.colour][phase - 1] == "d"):
            return
        far, distance, sign = SIZES[axis] // 2, abs(offset), 1 if offset > 0 else -1
        if distance < far - 1:
            send(now, actions, got, axis, sign, phase, offset + sign, 2)
        elif distance == far - 1:
            if phase == 1:
                if sign == (1 if (got.wave + got.colour) % 2 else -1):
                    send(now, actions, got, axis, sign, phase, far, 2)
            else:
                part = got.cut(COLOURS[got.colour][0][0], 0 if sign == 1 else 1)
                send(now, actions, part, axis, sign, phase, far, 1)

    for wave in range(WAVES):
        heapq.heappush(heap, (READY[wave], -9 + wave, None, None, 0, wave, None, None))
    while heap:
        waiting.sort(key=lambda w: (w[1], CHUNKS.index(w[2])))
        ripe = [w for w in waiting if max(w[0], core) <= heap[0][0] and turn[0] == w[1:]]
        if ripe:
            waiting.remove(ripe[0])
            turn.pop(0)
            order.append((max(ripe[0][0], core), "product", ripe[0][1], ripe[0][2], None, None, None))
            core = max(ripe[0][0], core) + CHUNK
            continue
        now, index, got, axis, phase, step, offset, weight = heapq.heappop(heap)
        now = max(now, core)
        actions, local = [], []
        if phase == 0:
            wave = step
            for colour in range(3):
                start(now, actions, Piece(wave, colour, dict(x=0, y=0, z=0)), COLOURS[colour][0][0], 1)
            order.append((now, "ready", wave, None, actions, local, None))
            continue
        wave, colour = got.wave, got.colour
        a, b, c = COLOURS[colour][0]
        forward(now, actions, got, axis, phase, offset, weight)
        if phase == 1:
            tag = (wave, colour)
            arrived[tag] = arrived.get(tag, 0) + 1
            if arrived[tag] == SIZES[a] - 1:
                line = Piece(wave, colour, {a: (0, SIZES[a]), b: 0, c: 0})
                start(now, actions, line, b, 2)
                start(now, actions, line, c, 3)
                local.append(line)
        else:
            full = Piece(wave, colour, {**got.where, a: (0, SIZES[a])})
            tag = (phase, full.key())
            arrived[tag] = arrived.get(tag, 0) + weight
            if arrived[tag] == 2:
                if phase == 2:
                    start(now, actions, full, c, 3)
                local.append(full)
        for piece in local:
            landed(now, wave, piece)
        order.append((now, "recv", wave, got, actions, local, index))
    for time, wave, chunk in sorted(waiting, key=lambda w: (w[1], CHUNKS.index(w[2]))):
        core = max(core, now, time) + CHUNK
        order.append((core, "product", wave, chunk, None, None, None))
    return order, serial[0]


PLAN, COPIES = make_plan()
PAIRS = [piece for event in PLAN if event[1] == "recv" for piece in event[5]]
PAIR_INDEX = {piece.key(): index for index, piece in enumerate(PAIRS)}


def kernel(fast_in, slow_in, moment_in, tokens_in, gain_in,
           slow_new, moment_new, fast_new, key_values,
           tiles, fast, outgoing, incoming, slow, moment, tokens, gain, total,
           load_sem, rs_send, rs_recv, ag_send, ag_recv, pair_send, pair_recv):
    outer, dp = lax.axis_index("outer"), lax.axis_index("dp")
    x, yh = outer // 2, outer % 2
    yl, z, core = dp // 16, (dp // 2) % NZ, dp % 2
    y = yh * 2 + yl
    here = dict(x=x, y=y, z=z)
    other = 1 - core

    def device(px, py, pz, pc):
        return (px * 2 + py // 2, (py % 2) * 16 + pz * 2 + pc)

    def beside(axis, step):
        at = dict(here)
        at[axis] = lax.rem(at[axis] + (step % SIZES[axis]), SIZES[axis])
        return device(at["x"], at["y"], at["z"], core)

    partner = device(x, y, z, other)

    loads = [
        pltpu.make_async_copy(fast_in.at[0], fast, load_sem.at[0]),
        pltpu.make_async_copy(slow_in, slow, load_sem.at[1]),
        pltpu.make_async_copy(moment_in, moment, load_sem.at[2]),
        pltpu.make_async_copy(gain_in, gain, load_sem.at[3]),
        pltpu.make_async_copy(tokens_in, tokens, load_sem.at[4]),
    ]
    for load in loads:
        load.start()

    peers = []
    for dx in range(NX):
        for dy in (0, 2):
            if dx or dy:
                peers.append(device(lax.rem(x + dx, NX), lax.rem(y + dy, NY), z, core))
    greet = list(peers) + [partner, beside("y", 1), beside("y", -1)] + [beside("z", s) for s in range(1, NZ)]
    barrier = pltpu.get_barrier_semaphore()
    for peer in greet:
        pl.semaphore_signal(barrier, inc=1, device_id=peer, device_id_type=MESH)

    loads[0].wait()
    for wave in range(WAVES):
        for o in range(NX * 2):
            outgoing[wave, o] = fast[:, o * 256 + wave * LANES:o * 256 + (wave + 1) * LANES].astype(jnp.bfloat16)
    loads[1].wait()
    loads[2].wait()
    loads[3].wait()
    pl.semaphore_wait(barrier, len(greet))

    for wave in range(WAVES):
        for index, peer in enumerate(peers):
            pltpu.make_async_remote_copy(
                src_ref=outgoing.at[wave, peer[0]], dst_ref=incoming.at[wave, outer],
                send_sem=rs_send.at[wave], recv_sem=rs_recv.at[wave], device_id=peer, device_id_type=MESH).start()

    def norm_rows(first, count):
        @pl.loop(first, first + count)
        def _(i):
            rows = pl.ds(i * 16, 16)
            values = tokens[rows, :].astype(jnp.float32)
            meansq = jnp.mean(values * values, axis=-1, keepdims=True)
            tokens[rows, :] = (values * lax.rsqrt(meansq + EPSILON) * gain[...]).astype(jnp.bfloat16)

    def rs_wait(wave):
        landed = incoming.at[wave, 0:7]
        pltpu.make_async_remote_copy(
            src_ref=landed, dst_ref=landed, send_sem=rs_send.at[wave], recv_sem=rs_recv.at[wave],
            device_id=partner, device_id_type=MESH).wait_recv()

    def update(wave):
        cols = slice(wave * LANES, (wave + 1) * LANES)
        summed = fast[:, pl.ds(pl.multiple_of(outer * 256 + wave * LANES, LANES), LANES)]
        for k in range(1, NX * 2):
            summed = summed + incoming[wave, lax.rem(outer + k, NX * 2)].astype(jnp.float32)
        part = slow[:, cols]
        outer_grad = part - summed / (NX * 2)
        moment_next = MOMENTUM_COEF * moment[:, cols] + outer_grad
        slow_next = part - OUTER_LR * (outer_grad + MOMENTUM_COEF * moment_next)
        tiles[wave, x, y, z, core] = slow_next.astype(jnp.bfloat16)
        slow_new[:, cols] = slow_next
        moment_new[:, cols] = moment_next

    def slice_of(piece, parity):
        lo, hi = COLOURS[piece.colour][1 + piece.wave]
        index = [piece.wave]
        for axis in ("x", "y", "z"):
            span = piece.where[axis]
            if isinstance(span, tuple):
                index.append(slice(span[0], span[1]))
            else:
                index.append(lax.rem(here[axis] + span, SIZES[axis]) if span else here[axis])
        return tiles.at[(*index, parity, slice(lo, hi), slice(None))]

    def ag_copy(piece, axis, step, phase, index):
        ref = slice_of(piece, core)
        return pltpu.make_async_remote_copy(
            src_ref=ref, dst_ref=ref, send_sem=ag_send.at[piece.wave, piece.colour, phase - 1], recv_sem=ag_recv.at[index],
            device_id=beside(axis, step), device_id_type=MESH)

    def pair_copy(piece, parity):
        ref = slice_of(piece, parity)
        return pltpu.make_async_remote_copy(
            src_ref=ref, dst_ref=ref, send_sem=pair_send.at[piece.wave], recv_sem=pair_recv.at[PAIR_INDEX[piece.key()]],
            device_id=partner, device_id_type=MESH)

    collected = set()

    def collect(wave, needed):
        for piece in PAIRS:
            if piece.wave == wave and piece.key() not in collected and needed & set(piece.tiles()):
                collected.add(piece.key())
                pair_copy(piece, other).wait_recv()

    def matmul(k):
        wave, q = k // len(CHUNKS), k % len(CHUNKS)
        turn, pair = q // 2, q % 2
        dy = jnp.where(turn == 0, 0, jnp.where(turn == 1, 3, jnp.where(turn == 2, 1, 2)))
        py = lax.rem(y + dy, NY)
        half = py // 2
        pxs = [lax.rem(x + dx, NX) for dx in (3 * pair, 1 + pair)]
        deep = pl.ds(pl.multiple_of((py % 2) * 2048, 2048), 2048)

        def each(m):
            rows = pl.ds(pl.multiple_of(m * (768 // STEPS), 768 // STEPS), 768 // STEPS)
            weights = jnp.concatenate([tiles[wave, px, py].reshape(2048, LANES) for px in pxs], axis=1)
            total[pair, half, rows] += jnp.dot(tokens[rows, deep], weights, preferred_element_type=jnp.float32)

        if STEPS == 1:
            each(0)
        else:
            pl.loop(0, STEPS)(each)

        @pl.when(turn >= 2)
        def _():
            full = jnp.where(turn == 2, yh, 1 - yh)

            @pl.loop(0, 6)
            def _(m):
                rows = pl.ds(pl.multiple_of(m * 128, 128), 128)
                value = (total[pair, full, rows] * (4096 ** -0.5)).astype(jnp.bfloat16)
                total[pair, full, rows] = jnp.zeros((128, 256), jnp.float32)
                for side, px in enumerate(pxs):
                    first = pl.multiple_of((px * 2 + full) * 256 + wave * LANES, LANES)
                    key_values[rows, pl.ds(first, LANES)] = value[:, side * LANES:(side + 1) * LANES]

    def own_rows(wave):
        for o in range(NX * 2):
            cols = slice(o * 256 + wave * LANES, o * 256 + (wave + 1) * LANES)
            rounded = tiles[wave, o // 2, (o % 2) * 2 + yl, z, core].astype(jnp.float32)
            exact = slow_new[:, wave * LANES:(wave + 1) * LANES]
            fast_new[:, cols] = jnp.where(jnp.full((128, LANES), o, jnp.int32) == outer, exact, rounded)

    total[...] = jnp.zeros_like(total)
    loads[4].wait()
    norm_rows(0, 16)
    def step(event):
        now, kind, wave, got, actions, local, index = event
        if kind == "ready":
            rs_wait(wave)
            update(wave)
        else:
            ref = slice_of(got, core)
            pltpu.make_async_remote_copy(
                src_ref=ref, dst_ref=ref, send_sem=ag_send.at[0, 0, 0], recv_sem=ag_recv.at[index],
                device_id=partner, device_id_type=MESH).wait_recv()
        for action in actions:
            ag_copy(*action).start()
        for piece in local:
            pair_copy(piece, core).start()
        if kind == "ready":
            norm_rows(16 + 16 * wave, 16)

    groups = [[]]
    for event in PLAN:
        groups[-1].append(event)
        if event[1] == "product":
            groups.append([])
    for event in groups[0][:-1]:
        step(event)
    groups[0] = groups[0][-1:]

    @pl.loop(0, 2 * len(CHUNKS))
    def _(k):
        for number, group in enumerate(groups[:-1]):
            @pl.when(k == number)
            def _():
                for event in group[:-1]:
                    step(event)
                wave, (pair, dy) = group[-1][2:4]
                if number in (len(CHUNKS), 2 * len(CHUNKS) - 1):
                    own_rows(number // len(CHUNKS) - 1 if number == len(CHUNKS) else 1)
                collect(wave, {(dx, dy, dz) for dx in pair for dz in range(NZ)})

        matmul(k)

    for wave in range(WAVES):
        sent = incoming.at[wave, 0:7]
        pltpu.make_async_remote_copy(
            src_ref=sent, dst_ref=sent, send_sem=rs_send.at[wave], recv_sem=rs_recv.at[wave],
            device_id=partner, device_id_type=MESH).wait_send()
        sent = tiles.at[wave, :, :, :, core]
        pltpu.make_async_remote_copy(
            src_ref=sent, dst_ref=sent, send_sem=pair_send.at[wave], recv_sem=pair_recv.at[0],
            device_id=partner, device_id_type=MESH).wait_send()
        for colour, (axes, *_r) in enumerate(COLOURS):
            lo, hi = COLOURS[colour][1 + wave]
            a, b, c = axes
            ranges = (
                {a: slice(0, SIZES[a] - 1), b: 0, c: 0},
                {a: slice(0, SIZES[a]), b: slice(0, SIZES[b] - 1), c: 0},
                {a: slice(0, SIZES[a]), b: slice(0, SIZES[b]), c: slice(0, SIZES[c] - 1)},
            )
            for phase, span in enumerate(ranges):
                sent = tiles.at[wave, span["x"], span["y"], span["z"], core, lo:hi, :]
                pltpu.make_async_remote_copy(
                    src_ref=sent, dst_ref=sent, send_sem=ag_send.at[wave, colour, phase], recv_sem=ag_recv.at[0],
                    device_id=partner, device_id_type=MESH).wait_send()


def keep(slow_new, moment_new, fast_new, key_values, slow_out, moment_out, fast_out, kv_out, sem):
    copies = []
    count = key_values.shape[0]
    for q in range(4):
        rows = slice(q * count // 4, (q + 1) * count // 4)
        copies.append(pltpu.make_async_copy(key_values.at[rows], kv_out.at[rows], sem.at[q]))
    copies.append(pltpu.make_async_copy(fast_new, fast_out, sem.at[4]))
    copies.append(pltpu.make_async_copy(slow_new, slow_out, sem.at[5]))
    copies.append(pltpu.make_async_copy(moment_new, moment_out, sem.at[6]))
    for copy in copies:
        copy.start()
    for copy in copies:
        copy.wait()


def body(fast_weights, slow_weights, momentum, tokens, norm_gain):
    rows, cols = slow_weights.shape
    count, width = tokens.shape
    whole = fast_weights.shape[2]
    hbm = pl.BlockSpec(memory_space=pltpu.HBM)
    dma = pltpu.SemaphoreType.DMA
    made = pl.pallas_call(
        kernel,
        out_shape=(
            jax.ShapeDtypeStruct((rows, cols), jnp.float32),
            jax.ShapeDtypeStruct((rows, cols), jnp.float32),
            jax.ShapeDtypeStruct((rows, whole), jnp.float32),
            jax.ShapeDtypeStruct((count, whole), jnp.bfloat16),
        ),
        in_specs=[hbm] * 5,
        out_specs=(pl.BlockSpec(memory_space=pltpu.VMEM),) * 4,
        scratch_shapes=[
            pltpu.VMEM((WAVES, NX, NY, NZ, 2, 128, LANES), jnp.bfloat16),
            pltpu.VMEM((rows, whole), jnp.float32),
            pltpu.VMEM((WAVES, 8, rows, LANES), jnp.bfloat16),
            pltpu.VMEM((WAVES, 8, rows, LANES), jnp.bfloat16),
            pltpu.VMEM((rows, cols), jnp.float32),
            pltpu.VMEM((rows, cols), jnp.float32),
            pltpu.VMEM((count, width), jnp.bfloat16),
            pltpu.VMEM((1, width), jnp.float32),
            pltpu.VMEM((2, 2, count, 256), jnp.float32),
            dma((5,)),
            dma((WAVES,)),
            dma((WAVES,)),
            dma((WAVES, 3, 3)),
            dma((COPIES,)),
            dma((WAVES,)),
            dma((len(PAIRS),)),
        ],
        compiler_params=pltpu.CompilerParams(collective_id=0, has_side_effects=True, vmem_limit_bytes=48 * 1024 * 1024),
    )(fast_weights, slow_weights, momentum, tokens, norm_gain.reshape(1, width))
    return pl.pallas_call(
        keep,
        out_shape=tuple(jax.ShapeDtypeStruct(m.shape, m.dtype) for m in made),
        in_specs=[pl.BlockSpec(memory_space=pl.ANY)] * 4,
        out_specs=(hbm,) * 4,
        scratch_shapes=[dma((8,))],
        compiler_params=pltpu.CompilerParams(vmem_limit_bytes=1024 * 1024),
    )(*made)


def solution(mesh):
    in_specs = (
        P("outer", "dp", None),
        P("dp", "outer"),
        P("dp", "outer"),
        P(("outer", "dp"), None),
        P(),
    )
    out_specs = (P("dp", "outer"), P("dp", "outer"), P("dp", None), P(("outer", "dp"), None))
    return jax.shard_map(body, mesh=mesh, in_specs=in_specs, out_specs=out_specs, check_vma=False)
```

time: 102 us -> 79.8 us (0.78)
  Pallas kernels: 91.5 us -> 75.2 us
  local copies, waits for them, and re-layouts: 9.4 us -> 3.74 us
    pallas_call x1, Pallas kernels: 91.5 us -> 73.1 us  [body(): pl.pallas_call(kernel, out_shape=(jax.ShapeDtypeStruct((rows, cols), jnp....]
    unnamed x4 -> x8, local copies, waits for them, and re-layouts: 9.4 us -> 3.74 us
    pallas_call x0 -> x1, Pallas kernels: none -> 2.15 us  [body(): pl.pallas_call(keep, out_shape=tuple((jax.ShapeDtypeStruct(m.shape, m.dty...]
where the time goes in v2:
time: 79.8 us; the launch traced here: 79.6 us
  Pallas kernels  75.2 us (94%)
  local copies, waits for them, and re-layouts  3.74 us (5%)
    pallas_call x1, Pallas kernels, body(): pl.pallas_call(kernel, out_shape=(jax.ShapeDtypeStruct((rows, cols), jnp....  73.1 us
    unnamed x8, local copies, waits for them, and re-layouts  3.74 us
    pallas_call x1, Pallas kernels, body(): pl.pallas_call(keep, out_shape=tuple((jax.ShapeDtypeStruct(m.shape, m.dty...  2.15 us

profile of v2, /device:TPU:1, one launch (start us, length us, event | category | flops | bytes accessed | tf_op | source)
XLA Modules:
  0.0 79.6 jit_solution(3867100915544382011)
XLA Ops:
  0.6 0.0 copy-start
  0.6 1.2 %copy-done = f32[1,128,2048]{2,1,0:T(8,128)S(1)} copy-done((f32[1,128,2048]{2,1,0:T(8,128)S(1)}, f32[1,128,2048]{2,1,0:T(8,128)}, u32[]{:S(2)}) %copy-start) | copy-done | bytes 1048600
  1.9 0.0 copy-start.1
  1.9 0.9 %copy-done.1 = f32[128,256]{1,0:T(8,128)S(1)} copy-done((f32[128,256]{1,0:T(8,128)S(1)}, f32[128,256]{1,0:T(8,128)}, u32[]{:S(2)}) %copy-start.1) | copy-done | bytes 131096
  2.8 0.0 copy-start.2
  2.8 0.9 %copy-done.2 = f32[128,256]{1,0:T(8,128)S(1)} copy-done((f32[128,256]{1,0:T(8,128)S(1)}, f32[128,256]{1,0:T(8,128)}, u32[]{:S(2)}) %copy-start.2) | copy-done | bytes 131096
  3.7 0.0 copy-start.3
  3.7 0.7 copy-done.3
  4.4 73.1 %shard_map.84 = (f32[128,256]{1,0:T(8,128)S(1)}, f32[128,256]{1,0:T(8,128)S(1)}, f32[128,2048]{1,0:T(8,128)S(1)}, bf16[768,2048]{1,0:T(8,128)(2,1)S(1)}) custom-call(f32[1,128,2048]{2,1,0:T(8,128)S(1)} %copy-done, f32[128,256]{1,0:T(8,128)S(1)} %copy-done.1, f32[128,256]{1,0:T(8,128)S(1)} %copy-done.2, bf16[768,4096]{1,0:T(8,128)(2,1)} %tokens_in.1, ...), custom_call_target="tpu_custom_call" | custom-call | tf_op jit(solution)/shard_map/pallas_call | solution.py:423
  77.5 2.1 %shard_map.85 = (f32[128,256]{1,0:T(8,128)}, f32[128,256]{1,0:T(8,128)}, f32[128,2048]{1,0:T(8,128)}, bf16[768,2048]{1,0:T(8,128)(2,1)}) custom-call(f32[128,256]{1,0:T(8,128)S(1)} %get-tuple-element.8.slow_new, f32[128,256]{1,0:T(8,128)S(1)} %get-tuple-element.9.moment_new, f32[128,2048]{1,0:T(8,128)S(1)} %get-tuple-element.10.fast_new, ...), custom_call_target="tpu_custom_call" | custom-call | tf_op jit(solution)/shard_map/pallas_call | solution.py:453
Async XLA Ops:
  0.6 1.2 %copy-start = (f32[1,128,2048]{2,1,0:T(8,128)S(1)}, f32[1,128,2048]{2,1,0:T(8,128)}, u32[]{:S(2)}) copy-start(f32[1,128,2048]{2,1,0:T(8,128)} %fast_in.1) | copy-start | bytes 3145732
  1.9 0.9 %copy-start.1 = (f32[128,256]{1,0:T(8,128)S(1)}, f32[128,256]{1,0:T(8,128)}, u32[]{:S(2)}) copy-start(f32[128,256]{1,0:T(8,128)} %slow_in.1) | copy-start | bytes 393220
  2.8 0.9 %copy-start.2 = (f32[128,256]{1,0:T(8,128)S(1)}, f32[128,256]{1,0:T(8,128)}, u32[]{:S(2)}) copy-start(f32[128,256]{1,0:T(8,128)} %moment_in.1) | copy-start | bytes 393220
  3.7 0.7 copy-start.3

commit v3 on v2

--- a/solution.py
+++ b/solution.py
@@ -19,10 +19,10 @@
 LANES = 128
 COLOURS = (
     (("x", "y", "z"), (0, 48), (0, 32)),
-    (("z", "y", "x"), (48, 80), (32, 80)),
-    (("z", "x", "y"), (80, 128), (80, 128)),
+    (("z", "x", "y"), (48, 80), (32, 96)),
+    (("z", "y", "x"), (80, 128), (96, 128)),
 )
-MODES = (("dr", "dr", "dr"), ("dr", "dr", "dr"))
+MODES = (("dr", "dr", "dr"), ("rr", "dr", "dr"))
 LINK = 45.5
 HOP, FURTHER = 2.7, 0.75
 READY = (0.0, 4.5)
@@ -179,9 +179,9 @@
 PAIR_INDEX = {piece.key(): index for index, piece in enumerate(PAIRS)}
 
 
-def kernel(fast_in, slow_in, moment_in, tokens_in, gain_in,
+def kernel(fast, packed, tokens_in,
            slow_new, moment_new, fast_new, key_values,
-           tiles, fast, outgoing, incoming, slow, moment, tokens, gain, total,
+           tiles, outgoing, incoming, tokens, gain, total,
            load_sem, rs_send, rs_recv, ag_send, ag_recv, pair_send, pair_recv):
     outer, dp = lax.axis_index("outer"), lax.axis_index("dp")
     x, yh = outer // 2, outer % 2
@@ -200,15 +200,12 @@
 
     partner = device(x, y, z, other)
 
-    loads = [
-        pltpu.make_async_copy(fast_in.at[0], fast, load_sem.at[0]),
-        pltpu.make_async_copy(slow_in, slow, load_sem.at[1]),
-        pltpu.make_async_copy(moment_in, moment, load_sem.at[2]),
-        pltpu.make_async_copy(gain_in, gain, load_sem.at[3]),
-        pltpu.make_async_copy(tokens_in, tokens, load_sem.at[4]),
-    ]
-    for load in loads:
-        load.start()
+    load = pltpu.make_async_copy(tokens_in, tokens, load_sem.at[0])
+    load.start()
+    deep, wide = 128, 256
+    slow, moment = packed.at[0:deep], packed.at[deep:2 * deep]
+    for r in range(4096 // wide):
+        gain[0:1, r * wide:(r + 1) * wide] = packed[2 * deep + r:2 * deep + r + 1, :]
 
     peers = []
     for dx in range(NX):
@@ -220,16 +217,14 @@
     for peer in greet:
         pl.semaphore_signal(barrier, inc=1, device_id=peer, device_id_type=MESH)
 
-    loads[0].wait()
     for wave in range(WAVES):
-        for o in range(NX * 2):
-            outgoing[wave, o] = fast[:, o * 256 + wave * LANES:o * 256 + (wave + 1) * LANES].astype(jnp.bfloat16)
-    loads[1].wait()
-    loads[2].wait()
-    loads[3].wait()
-    pl.semaphore_wait(barrier, len(greet))
-
-    for wave in range(WAVES):
+        @pl.loop(0, NX * 2)
+        def _(o):
+            cols = pl.ds(pl.multiple_of(o * 256 + wave * LANES, LANES), LANES)
+            outgoing[wave, o] = fast[0, :, cols].astype(jnp.bfloat16)
+
+        if wave == 0:
+            pl.semaphore_wait(barrier, len(greet))
         for index, peer in enumerate(peers):
             pltpu.make_async_remote_copy(
                 src_ref=outgoing.at[wave, peer[0]], dst_ref=incoming.at[wave, outer],
@@ -251,7 +246,7 @@
 
     def update(wave):
         cols = slice(wave * LANES, (wave + 1) * LANES)
-        summed = fast[:, pl.ds(pl.multiple_of(outer * 256 + wave * LANES, LANES), LANES)]
+        summed = fast[0, :, pl.ds(pl.multiple_of(outer * 256 + wave * LANES, LANES), LANES)]
         for k in range(1, NX * 2):
             summed = summed + incoming[wave, lax.rem(outer + k, NX * 2)].astype(jnp.float32)
         part = slow[:, cols]
@@ -326,14 +321,16 @@
                     key_values[rows, pl.ds(first, LANES)] = value[:, side * LANES:(side + 1) * LANES]
 
     def own_rows(wave):
-        for o in range(NX * 2):
-            cols = slice(o * 256 + wave * LANES, o * 256 + (wave + 1) * LANES)
-            rounded = tiles[wave, o // 2, (o % 2) * 2 + yl, z, core].astype(jnp.float32)
-            exact = slow_new[:, wave * LANES:(wave + 1) * LANES]
-            fast_new[:, cols] = jnp.where(jnp.full((128, LANES), o, jnp.int32) == outer, exact, rounded)
+        @pl.loop(0, NX * 2)
+        def _(o):
+            cols = pl.ds(pl.multiple_of(o * 256 + wave * LANES, LANES), LANES)
+            fast_new[:, cols] = tiles[wave, o // 2, (o % 2) * 2 + yl, z, core].astype(jnp.float32)
+
+        cols = pl.ds(pl.multiple_of(outer * 256 + wave * LANES, LANES), LANES)
+        fast_new[:, cols] = slow_new[:, wave * LANES:(wave + 1) * LANES]
 
     total[...] = jnp.zeros_like(total)
-    loads[4].wait()
+    load.wait()
     norm_rows(0, 16)
     def step(event):
         now, kind, wave, got, actions, local, index = event
@@ -361,18 +358,34 @@
         step(event)
     groups[0] = groups[0][-1:]
 
+    def arrive(number):
+        group = groups[number]
+        for event in group[:-1]:
+            step(event)
+        wave, (pair, dy) = group[-1][2:4]
+        if number == len(CHUNKS):
+            own_rows(0)
+        if number == 2 * len(CHUNKS) - 1:
+            own_rows(1)
+        collect(wave, {(dx, dy, dz) for dx in pair for dz in range(NZ)})
+
+    def branch(k, first, last):
+        if last - first == 1:
+            arrive(first)
+            return
+        middle = (first + last) // 2
+
+        @pl.when(k < middle)
+        def _():
+            branch(k, first, middle)
+
+        @pl.when(k >= middle)
+        def _():
+            branch(k, middle, last)
+
     @pl.loop(0, 2 * len(CHUNKS))
     def _(k):
-        for number, group in enumerate(groups[:-1]):
-            @pl.when(k == number)
-            def _():
-                for event in group[:-1]:
-                    step(event)
-                wave, (pair, dy) = group[-1][2:4]
-                if number in (len(CHUNKS), 2 * len(CHUNKS) - 1):
-                    own_rows(number // len(CHUNKS) - 1 if number == len(CHUNKS) else 1)
-                collect(wave, {(dx, dy, dz) for dx in pair for dz in range(NZ)})
-
+        branch(k, 0, len(groups) - 1)
         matmul(k)
 
     for wave in range(WAVES):
@@ -419,7 +432,9 @@
     count, width = tokens.shape
     whole = fast_weights.shape[2]
     hbm = pl.BlockSpec(memory_space=pltpu.HBM)
+    vmem = pl.BlockSpec(memory_space=pltpu.VMEM)
     dma = pltpu.SemaphoreType.DMA
+    packed = jnp.concatenate([slow_weights, momentum, norm_gain.reshape(-1, cols)], axis=0)
     made = pl.pallas_call(
         kernel,
         out_shape=(
@@ -428,19 +443,16 @@
             jax.ShapeDtypeStruct((rows, whole), jnp.float32),
             jax.ShapeDtypeStruct((count, whole), jnp.bfloat16),
         ),
-        in_specs=[hbm] * 5,
+        in_specs=[vmem, vmem, hbm],
         out_specs=(pl.BlockSpec(memory_space=pltpu.VMEM),) * 4,
         scratch_shapes=[
             pltpu.VMEM((WAVES, NX, NY, NZ, 2, 128, LANES), jnp.bfloat16),
-            pltpu.VMEM((rows, whole), jnp.float32),
             pltpu.VMEM((WAVES, 8, rows, LANES), jnp.bfloat16),
             pltpu.VMEM((WAVES, 8, rows, LANES), jnp.bfloat16),
-            pltpu.VMEM((rows, cols), jnp.float32),
-            pltpu.VMEM((rows, cols), jnp.float32),
             pltpu.VMEM((count, width), jnp.bfloat16),
             pltpu.VMEM((1, width), jnp.float32),
             pltpu.VMEM((2, 2, count, 256), jnp.float32),
-            dma((5,)),
+            dma((1,)),
             dma((WAVES,)),
             dma((WAVES,)),
             dma((WAVES, 3, 3)),
@@ -449,7 +461,7 @@
             dma((len(PAIRS),)),
         ],
         compiler_params=pltpu.CompilerParams(collective_id=0, has_side_effects=True, vmem_limit_bytes=48 * 1024 * 1024),
-    )(fast_weights, slow_weights, momentum, tokens, norm_gain.reshape(1, width))
+    )(fast_weights, packed, tokens)
     return pl.pallas_call(
         keep,
         out_shape=tuple(jax.ShapeDtypeStruct(m.shape, m.dtype) for m in made),

time: 79.8 us -> 75.8 us (0.950)
  Pallas kernels: 75.2 us -> 72 us
  local copies, waits for them, and re-layouts: 3.74 us -> 1.94 us
  other arithmetic: 0 us -> 0.99 us
    pallas_call x1, Pallas kernels: 73.1 us -> 69.8 us  [body(): pl.pallas_call(kernel, out_shape=(jax.ShapeDtypeStruct((rows, cols), jnp....]
    unnamed x8 -> x2, local copies, waits for them, and re-layouts: 3.74 us -> 1.22 us
    concatenate x0 -> x1, other arithmetic: none -> 0.99 us  [body(): jnp.concatenate([slow_weights, momentum, norm_gain.reshape(-1, cols)], ax...]
where the time goes in v3:
time: 75.8 us; the launch traced here: 75.5 us
  Pallas kernels  72 us (95%)
  local copies, waits for them, and re-layouts  1.94 us (3%)
  other arithmetic  0.99 us (1%)
    pallas_call x1, Pallas kernels, body(): pl.pallas_call(kernel, out_shape=(jax.ShapeDtypeStruct((rows, cols), jnp....  69.8 us
    pallas_call x1, Pallas kernels, body(): pl.pallas_call(keep, out_shape=tuple((jax.ShapeDtypeStruct(m.shape, m.dty...  2.15 us

profile of v3, /device:TPU:1, one launch (start us, length us, event | category | flops | bytes accessed | tf_op | source)
XLA Modules:
  0.0 75.5 jit_solution(2197328130343833607)
XLA Ops:
  0.6 0.7 reshape.11
  1.4 1.0 %pad_maximum_fusion.packed = f32[272,256]{1,0:T(8,128)S(1)} fusion(f32[16,256]{1,0:T(8,128)S(1)} %reshape.11, f32[128,256]{1,0:T(8,128)} %param.7, f32[128,256]{1,0:T(8,128)} %param.6), kind=kLoop, calls=%fused_computation | loop fusion | flops 139264 | bytes 557056 | tf_op jit(solution)/shard_map/concatenate | solution.py:437
  2.3 0.0 copy-start
  2.4 1.2 %copy-done = f32[1,128,2048]{2,1,0:T(8,128)S(1)} copy-done((f32[1,128,2048]{2,1,0:T(8,128)S(1)}, f32[1,128,2048]{2,1,0:T(8,128)}, u32[]{:S(2)}) %copy-start) | copy-done | bytes 1048600
  3.6 69.8 %shard_map.84 = (f32[128,256]{1,0:T(8,128)S(1)}, f32[128,256]{1,0:T(8,128)S(1)}, f32[128,2048]{1,0:T(8,128)S(1)}, bf16[768,2048]{1,0:T(8,128)(2,1)S(1)}) custom-call(f32[1,128,2048]{2,1,0:T(8,128)S(1)} %copy-done, f32[272,256]{1,0:T(8,128)S(1)} %pad_maximum_fusion.packed, bf16[768,4096]{1,0:T(8,128)(2,1)} %tokens_in.1), custom_call_target="tpu_custom_call" | custom-call | tf_op jit(solution)/shard_map/pallas_call | solution.py:438
  73.4 2.1 %shard_map.85 = (f32[128,256]{1,0:T(8,128)}, f32[128,256]{1,0:T(8,128)}, f32[128,2048]{1,0:T(8,128)}, bf16[768,2048]{1,0:T(8,128)(2,1)}) custom-call(f32[128,256]{1,0:T(8,128)S(1)} %get-tuple-element.8.slow_new, f32[128,256]{1,0:T(8,128)S(1)} %get-tuple-element.9.moment_new, f32[128,2048]{1,0:T(8,128)S(1)} %get-tuple-element.10.fast_new, ...), custom_call_target="tpu_custom_call" | custom-call | tf_op jit(solution)/shard_map/pallas_call | solution.py:465
Async XLA Ops:
  2.3 1.2 %copy-start = (f32[1,128,2048]{2,1,0:T(8,128)S(1)}, f32[1,128,2048]{2,1,0:T(8,128)}, u32[]{:S(2)}) copy-start(f32[1,128,2048]{2,1,0:T(8,128)} %fast.1) | copy-start | bytes 3145732
